TPU v7x, 256 devices: a whole 4x4x8 slice. The times are simulated.
256 devices in a mesh: site: 4 (over y), rows: 4 (over z_lo), cols: 4 (over z_hi, core), slabs: 4 (over x).
Axes of the slice: x: 4, y: 4, z: 8 (z_hi: 2, z_lo: 4; z = z_hi * 4 + z_lo), core: 2. Of those that a mesh axis runs over, the one named last changes fastest.
Arguments:
- pressure: float32 [64, 256, 128, 128], P(('site', 'rows'), 'cols', 'slabs'), parts along dimension 0, may hold values from 0.2 to 1.8
- earlier: float32 [64, 256, 128, 128], P(('site', 'rows'), 'cols', 'slabs'), parts along dimension 0, may hold values from 0.2 to 1.8
- speed_square: float32 [64, 256, 128, 128], P(('site', 'rows'), 'cols', 'slabs'), parts along dimension 0, may hold values from 0.05 to 0.3
Outputs:
- potential: float32 [64, 256, 128, 128], P(('site', 'rows'), 'cols', 'slabs'), parts along dimension 0
- pressure_end: float32 [64, 256, 128, 128], P(('site', 'rows'), 'cols', 'slabs'), parts along dimension 0
There are 4 independent parts, one for each index of `site`. A program takes and returns all parts, laid end to end along the dimension named above; each array names one. Nothing has to cross between parts.
All inputs are finite; a program needn't handle non-finite values.
Results may differ from a plain program's by a relative error of at most 0.00002.
Values sent between devices are 32-bit elements; how exact they have to be, the bound alone decides.
No kernel may reach another device: no remote copies, remote signals or barrier semaphores. Data moves between devices by JAX's collectives and lax.ppermute only.
A program may use at most 192 MiB of HBM per device.

v0:
```python
import functools

import jax
import jax.numpy as jnp
from jax import lax
from jax.experimental import pallas as pl
from jax.experimental.pallas import tpu as pltpu
from jax.sharding import PartitionSpec as P


STEPS = 4
GRID_J = 16
WIDTHS = (32, 32)
WRAP = 16
GROUP = 8
PIECES = ((16, 16), (16, 8, 8))


def step_kernel(refs, *, start, width, total, place, final, has_dst):
    n = iter(range(len(refs)))

    def take():
        return refs[next(n)]

    around = start + width > total
    own = total - start if around else width
    p_hbm, e_hbm, c_hbm, lo_hbm, hi_hbm, klo_hbm, khi_hbm = (take() for _ in range(7))
    ilo_hbm, ihi_hbm = (take(), take()) if around else (None, None)
    if has_dst:
        take()
    if place and not final:
        take(), take()
    out_hbm = take()
    slab = (slice(None), pl.ds(place, width))
    if final:
        tot_hbm = [take() for _ in final]
    else:
        dn_hbm, up_hbm, kfirst_hbm, klast_hbm = (take() for _ in range(4))
        ifirst_hbm, ilast_hbm = (take(), take()) if around else (None, None)
    pbuf, ebuf, cbuf, rbuf, kbuf, psem, esem, csem, osem, rsem, ksem = (take() for _ in range(11))
    rows, depth = pbuf.shape[0], pbuf.shape[2]
    groups = width // GROUP

    def column_of(g):
        return lax.rem(start + GROUP * g, total)

    def shift_of(g):
        if not around:
            return 1
        if isinstance(g, int):
            return 1 if GROUP * g < own else 3
        return jnp.where(GROUP * g < own, 1, 3)

    def field(g, which):
        there = pl.ds(column_of(g), GROUP)
        src, buf, shift, sem = (
            (p_hbm, pbuf, shift_of(g), psem),
            (e_hbm, ebuf, 0, esem),
            (c_hbm, cbuf, 0, csem),
        )[which]
        return pltpu.make_async_copy(
            src.at[:, there], buf.at[:, pl.ds(GROUP * g + shift, GROUP)], sem.at[g]
        )

    def result(g):
        mine = pl.ds(GROUP * g, GROUP)
        return pltpu.make_async_copy(
            ebuf.at[:, mine], out_hbm.at[:, pl.ds(column_of(g), GROUP)], osem.at[g]
        )

    edge = pbuf.shape[1] - 1
    ends = [
        pltpu.make_async_copy(
            p_hbm.at[:, pl.ds(start - 1, 1)], pbuf.at[:, pl.ds(0, 1)], ksem.at[2]
        ),
        pltpu.make_async_copy(
            p_hbm.at[:, pl.ds((start + width) % total, 1)],
            pbuf.at[:, pl.ds(edge, 1)],
            ksem.at[3],
        ),
        pltpu.make_async_copy(klo_hbm.at[slab], kbuf.at[0], ksem.at[0]),
        pltpu.make_async_copy(khi_hbm.at[slab], kbuf.at[1], ksem.at[1]),
        pltpu.make_async_copy(lo_hbm, rbuf.at[0], rsem.at[0]),
        pltpu.make_async_copy(hi_hbm, rbuf.at[1], rsem.at[1]),
    ]
    if around:
        ends += [
            pltpu.make_async_copy(ihi_hbm, pbuf.at[:, pl.ds(own + 1, 1)], ksem.at[8]),
            pltpu.make_async_copy(ilo_hbm, pbuf.at[:, pl.ds(own + 2, 1)], ksem.at[9]),
        ]
    for which in range(3):
        field(0, which).start()
    for cp in ends:
        cp.start()
    for g in range(1, groups):
        for which in range(3):
            field(g, which).start()
    k = lax.broadcasted_iota(jnp.int32, (depth, pbuf.shape[3]), 0)
    is_first, is_last = k == 0, k == depth - 1
    for cp in ends:
        cp.wait()
    field(0, 0).wait()

    def group(g, _):
        @pl.when(g + 1 < groups)
        def _():
            field(g + 1, 0).wait()

        field(g, 1).wait()
        field(g, 2).wait()

        def column(n, _):
            i = GROUP * g + n
            at = i + shift_of(g)
            mid = [pbuf[j, at] for j in range(rows)]
            acc = None
            for j in range(rows):
                x = mid[j]
                low = rbuf[0, i] if j == 0 else mid[j - 1]
                high = rbuf[1, i] if j == rows - 1 else mid[j + 1]
                below = jnp.where(is_first, kbuf[0, j, pl.ds(i, 1), :], pltpu.roll(x, 1, 0))
                above = jnp.where(
                    is_last, kbuf[1, j, pl.ds(i, 1), :], pltpu.roll(x, depth - 1, 0)
                )
                spread = (
                    low + high + pbuf[j, at - 1] + pbuf[j, at + 1] + below + above - 6.0 * x
                )
                new = 2.0 * x - ebuf[j, i] + cbuf[j, i] * spread
                ebuf[j, i] = new
                if final:
                    acc = new if acc is None else acc + new
                else:
                    kbuf[2, j, pl.ds(i, 1), :] = new[0:1]
                    kbuf[3, j, pl.ds(i, 1), :] = new[depth - 1 : depth]
            if final:
                rbuf[2, i] = acc
            return 0

        lax.fori_loop(0, GROUP, column, 0)
        result(g).start()
        return 0

    lax.fori_loop(0, groups, group, 0)
    if final:
        edges = [
            pltpu.make_async_copy(
                rbuf.at[2, pl.ds(sum(final[:a]), final[a])], tot_hbm[a], rsem.at[2 + a]
            )
            for a in range(len(final))
        ]
    else:
        edges = [
            pltpu.make_async_copy(ebuf.at[0], dn_hbm, rsem.at[2]),
            pltpu.make_async_copy(ebuf.at[rows - 1], up_hbm, rsem.at[3]),
            pltpu.make_async_copy(kbuf.at[2], kfirst_hbm.at[slab], ksem.at[4]),
            pltpu.make_async_copy(kbuf.at[3], klast_hbm.at[slab], ksem.at[5]),
        ]
        if around:
            edges += [
                pltpu.make_async_copy(ebuf.at[:, pl.ds(own, 1)], ifirst_hbm, ksem.at[6]),
                pltpu.make_async_copy(ebuf.at[:, pl.ds(own - 1, 1)], ilast_hbm, ksem.at[7]),
            ]
    for cp in edges:
        cp.start()
    for g in range(groups):
        result(g).wait()
    for cp in edges:
        cp.wait()


def step(p, e, c, halo, dst, slabs, *, start, width, place, final):
    rows, total, depth, lanes = p.shape
    around = start + width > total
    args = [p, e, c, *halo]
    aliases = {}
    has_dst = dst is not None and dst is not e
    if dst is not None and not has_dst:
        aliases = {1: 0}
    elif has_dst:
        aliases = {len(args): 0}
        args.append(dst)
    if place and not final:
        aliases = {**aliases, len(args): 3, len(args) + 1: 4}
        args += slabs
    f = jnp.float32
    outs = [jax.ShapeDtypeStruct(p.shape, f)]
    row = jax.ShapeDtypeStruct((width, depth, lanes), f)
    slab = jax.ShapeDtypeStruct((rows, total, lanes), f)
    col = jax.ShapeDtypeStruct((rows, 1, depth, lanes), f)
    if final:
        outs += [jax.ShapeDtypeStruct((part, depth, lanes), f) for part in final]
    else:
        outs += [row, row, slab, slab] + [col, col] * around
    groups = width // GROUP
    cells = rows * width * depth * lanes

    def body(*refs):
        step_kernel(
            refs,
            start=start,
            width=width,
            total=total,
            place=place,
            final=final,
            has_dst=has_dst,
        )

    hbm = pl.BlockSpec(memory_space=pltpu.HBM)
    return pl.pallas_call(
        body,
        out_shape=outs,
        in_specs=[hbm] * len(args),
        out_specs=[hbm] * len(outs),
        scratch_shapes=[
            pltpu.VMEM((rows, width + (4 if around else 2), depth, lanes), f),
            pltpu.VMEM((rows, width, depth, lanes), f),
            pltpu.VMEM((rows, width, depth, lanes), f),
            pltpu.VMEM((3 if final else 2, width, depth, lanes), f),
            pltpu.VMEM((4, rows, width, lanes), f),
        ]
        + [pltpu.SemaphoreType.DMA((groups,))] * 4
        + [pltpu.SemaphoreType.DMA((2 + max(2, len(final)),)), pltpu.SemaphoreType.DMA((10,))],
        input_output_aliases=aliases,
        cost_estimate=pl.CostEstimate(
            flops=cells * 40, bytes_accessed=cells * 16, transcendentals=0
        ),
        name="wave_step",
    )(*args)


def sums_kernel(p_hbm, *refs, start, widths, total, count, has_dst):
    pieces = len(widths)
    before_hbm = refs[: count * pieces]
    refs = refs[count * pieces + (1 if has_dst else 0) :]
    out_hbm, pbuf, bbuf, psem, osem, bsem = refs
    rows = pbuf.shape[0]
    groups = sum(widths) // GROUP

    def there(g):
        return pl.ds(lax.rem(start + GROUP * g, total), GROUP)

    def field(g):
        return pltpu.make_async_copy(
            p_hbm.at[:, there(g)], pbuf.at[:, pl.ds(GROUP * g, GROUP)], psem.at[g]
        )

    def result(g):
        return pltpu.make_async_copy(
            pbuf.at[:, pl.ds(GROUP * g, GROUP)], out_hbm.at[:, there(g)], osem.at[g]
        )

    carried = []
    for a, width in enumerate(widths):
        for s in range(count):
            carried.append(
                pltpu.make_async_copy(
                    before_hbm[a * count + s],
                    bbuf.at[s, pl.ds(sum(widths[:a]), width)],
                    bsem.at[a * count + s],
                )
            )
    for cp in carried:
        cp.start()
    for g in range(groups):
        field(g).start()
    for cp in carried:
        cp.wait()

    def group(g, _):
        field(g).wait()

        def column(n, _):
            i = GROUP * g + n
            acc = bbuf[0, i]
            for s in range(1, count):
                acc = acc + bbuf[s, i]
            for j in range(rows):
                acc = acc + pbuf[j, i]
                pbuf[j, i] = acc * (1.0 / GRID_J)
            return 0

        lax.fori_loop(0, GROUP, column, 0)
        result(g).start()
        return 0

    lax.fori_loop(0, groups, group, 0)
    for g in range(groups):
        result(g).wait()


def sums(p, before, dst, *, start, widths):
    rows, total, depth, lanes = p.shape
    count = len(before[0])
    args = [p] + [b for piece in before for b in piece]
    aliases = {}
    if dst is not None:
        aliases = {len(args): 0}
        args.append(dst)
    width = sum(widths)
    groups = width // GROUP
    cells = rows * width * depth * lanes
    hbm = pl.BlockSpec(memory_space=pltpu.HBM)
    return pl.pallas_call(
        functools.partial(
            sums_kernel,
            start=start,
            widths=widths,
            total=total,
            count=count,
            has_dst=dst is not None,
        ),
        out_shape=jax.ShapeDtypeStruct(p.shape, jnp.float32),
        in_specs=[hbm] * len(args),
        out_specs=hbm,
        scratch_shapes=[
            pltpu.VMEM((rows, width, depth, lanes), jnp.float32),
            pltpu.VMEM((count, width, depth, lanes), jnp.float32),
        ]
        + [pltpu.SemaphoreType.DMA((groups,))] * 2
        + [pltpu.SemaphoreType.DMA((count * len(widths),))],
        input_output_aliases=aliases,
        cost_estimate=pl.CostEstimate(
            flops=cells * 10, bytes_accessed=cells * 8, transcendentals=0
        ),
        name="running_sums",
    )(*args)


def ring(axis, by):
    size = lax.axis_size(axis)
    return [(a, (a + by) % size) for a in range(size)]


def local(pressure, earlier, speed_square):
    rows, total, depth, _ = pressure.shape
    starts = [(total - WRAP + sum(WIDTHS[:a])) % total for a in range(len(WIDTHS))]
    chunks = list(zip(starts, WIDTHS))

    def exchange(edges, a):
        dn, up, kfirst, klast = edges[:4]
        got = [
            lax.ppermute(up, "rows", ring("rows", 1)), lax.ppermute(dn, "rows", ring("rows", -1))
        ]
        if a == 0:
            ifirst, ilast = edges[4:]
            got += [
                lax.ppermute(ilast, "cols", ring("cols", 1)),
                lax.ppermute(ifirst, "cols", ring("cols", -1)),
            ]
        if a == len(chunks) - 1:
            got += [
                lax.ppermute(klast, "slabs", ring("slabs", 1)),
                lax.ppermute(kfirst, "slabs", ring("slabs", -1)),
            ]
        return got

    def start_edges(a):
        start, width = chunks[a]

        def part(value, start, width, axis):
            if start + width <= total:
                return lax.slice_in_dim(value, start, start + width, axis=axis)
            own = total - start
            return jnp.concatenate(
                [
                    lax.slice_in_dim(value, start, total, axis=axis),
                    lax.slice_in_dim(value, 0, width - own, axis=axis),
                ],
                axis=axis,
            )

        edges = [part(pressure[j], start, width, 0) for j in (0, rows - 1)]
        edges += [part(pressure[:, :, k], starts[0], total, 1) for k in (0, depth - 1)]
        if a == 0:
            edges += [pressure[:, :1], pressure[:, total - 1 :]]
        return edges

    halos = [exchange(start_edges(a), a) for a in range(len(chunks))]
    older, newer = earlier, pressure
    for t in range(STEPS):
        final = t == STEPS - 1
        fresh = None if t < 2 else older
        made, slabs = [], []
        for a, (start, width) in enumerate(chunks):
            before = older if t < 2 else fresh
            halo = halos[a][:2] + halos[-1][-2:] + (halos[0][2:4] if a == 0 else [])
            fresh, *edges = step(
                newer,
                before,
                speed_square,
                halo,
                fresh,
                slabs,
                start=start,
                width=width,
                place=sum(WIDTHS[:a]),
                final=PIECES[a] if final else (),
            )
            slabs = edges[2:4]
            made.append(edges if final else exchange(edges, a))
        older, newer = newer, fresh
        halos = made

    potential = None
    size = lax.axis_size("rows")
    for a, (start, width) in enumerate(chunks):
        carried_in = []
        for own in halos[a]:
            before, carried = [], own
            for s in range(size - 1):
                got = lax.ppermute(carried, "rows", [(s, s + 1)])
                before.append(got)
                carried = own + got
            carried_in.append(before)
        potential = sums(
            newer, carried_in, potential, start=start, widths=PIECES[a]
        )
    return potential, newer


def solution(mesh):
    placed = P(("site", "rows"), "cols", "slabs", None)

    return jax.shard_map(
        local,
        mesh=mesh,
        in_specs=(placed, placed, placed),
        out_specs=(placed, placed),
        check_vma=False,
    )
```

profile of v0, /device:TPU:1, one launch (start us, length us, event | category | flops | bytes accessed | tf_op | source)
XLA Modules:
  0.0 332.2 jit_solution(7083252928914048575)
XLA Ops:
  14.2 6.3 %collective-permute-start.6 = (f32[4,1,32,128]{3,2,1,0:T(8,128)S(1)}, f32[4,1,32,128]{3,2,1,0:T(8,128)S(1)}, u32[]{:S(2)}, u32[]{:S(2)}) collective-permute-start(f32[4,1,32,128]{3,2,1,0:T(8,128)S(1)} %get-tuple-element.89), channel_id=1, source_target_pairs={{0,4},{4,8},{8,12},{12,0},{1,5},{5,9},{9,13},{13,1},{2,6},{6,10},{... | collective-permute-start | bytes 196616 | tf_op jit(solution)/shard_map/ppermute | solution.py:347
  20.5 29.3 %collective-permute-done.6.refs_7_ = f32[4,1,32,128]{3,2,1,0:T(8,128)S(1)} collective-permute-done((f32[4,1,32,128]{3,2,1,0:T(8,128)S(1)}, f32[4,1,32,128]{3,2,1,0:T(8,128)S(1)}, u32[]{:S(2)}, u32[]{:S(2)}) %collective-permute-start.6) | collective-permute-done | bytes 65568 | tf_op jit(solution)/shard_map/ppermute | solution.py:347
  55.0 5.1 %collective-permute-done.2.refs_5_ = f32[4,64,128]{2,1,0:T(8,128)S(1)} collective-permute-done((f32[4,64,128]{2,1,0:T(8,128)S(1)}, f32[4,64,128]{2,1,0:T(8,128)S(1)}, u32[]{:S(2)}, u32[]{:S(2)}) %collective-permute-start.2) | collective-permute-done | bytes 131104 | tf_op jit(solution)/shard_map/ppermute | solution.py:352
  61.8 5.6 %wave_step.8 = (f32[4,64,32,128]{3,2,1,0:T(8,128)}, f32[32,32,128]{2,1,0:T(8,128)}, f32[32,32,128]{2,1,0:T(8,128)}, f32[4,64,128]{2,1,0:T(8,128)}, f32[4,64,128]...) custom-call(f32[4,64,32,128]{3,2,1,0:T(8,128)} %refs_1_.7, f32[4,64,32,128]{3,2,1,0:T(8,128)} %refs_1_.5, ...), custom_call_target="tpu_custom_call" | custom-call | flops 20971520 | bytes 8388608 | tf_op jit(solution)/shard_map/wave_step/pallas_call | solution.py:209
  67.5 3.8 %collective-permute-start.13 = (f32[32,32,128]{2,1,0:T(8,128)}, f32[32,32,128]{2,1,0:T(8,128)S(1)}, u32[]{:S(2)}, u32[]{:S(2)}) collective-permute-start(f32[32,32,128]{2,1,0:T(8,128)} %get-tuple-element.54), channel_id=1, source_target_pairs={{0,48},{16,0},{32,16},{48,32},{1,49},{17,1},{33,17},{49,33},{2,50}... | collective-permute-start | bytes 1572872 | tf_op jit(solution)/shard_map/ppermute | solution.py:342
  72.2 5.5 %wave_step.9 = (f32[4,64,32,128]{3,2,1,0:T(8,128)}, f32[32,32,128]{2,1,0:T(8,128)}, f32[32,32,128]{2,1,0:T(8,128)}, f32[4,64,128]{2,1,0:T(8,128)}, f32[4,64,128]{2,1,0:T(8,128)}) custom-call(f32[4,64,32,128]{3,2,1,0:T(8,128)} %refs_1_.7, f32[4,64,32,128]{3,2,1,0:T(8,128)} %refs_1_.5, ...), custom_call_target="tpu_custom_call", output_to_operand_aliasing={{0}: (7, {}), {3}: (8, {}), {4}: (9, {})} | custom-call | flops 20971520 | bytes 8388608 | tf_op jit(solution)/shard_map/wave_step/pallas_call | solution.py:209
  81.1 11.2 %collective-permute-start.14 = (f32[4,1,32,128]{3,2,1,0:T(8,128)S(1)}, f32[4,1,32,128]{3,2,1,0:T(8,128)S(1)}, u32[]{:S(2)}, u32[]{:S(2)}) collective-permute-start(f32[4,1,32,128]{3,2,1,0:T(8,128)S(1)} %copy-done.55), channel_id=1, source_target_pairs={{0,4},{4,8},{8,12},{12,0},{1,5},{5,9},{9,13},{13,1},{2,6},{6,10},{... | collective-permute-start | bytes 196616 | tf_op jit(solution)/shard_map/ppermute | solution.py:347
  92.2 10.4 %collective-permute-done.14.refs_7_ = f32[4,1,32,128]{3,2,1,0:T(8,128)S(1)} collective-permute-done((f32[4,1,32,128]{3,2,1,0:T(8,128)S(1)}, f32[4,1,32,128]{3,2,1,0:T(8,128)S(1)}, u32[]{:S(2)}, u32[]{:S(2)}) %collective-permute-start.14) | collective-permute-done | bytes 65568 | tf_op jit(solution)/shard_map/ppermute | solution.py:347
  102.7 22.0 %collective-permute-start.15 = (f32[4,1,32,128]{3,2,1,0:T(8,128)S(1)}, f32[4,1,32,128]{3,2,1,0:T(8,128)S(1)}, u32[]{:S(2)}, u32[]{:S(2)}) collective-permute-start(f32[4,1,32,128]{3,2,1,0:T(8,128)S(1)} %copy-done.52), channel_id=1, source_target_pairs={{0,12},{4,0},{8,4},{12,8},{1,13},{5,1},{9,5},{13,9},{2,14},{6,2},{... | collective-permute-start | bytes 196616 | tf_op jit(solution)/shard_map/ppermute | solution.py:348
  125.5 5.2 %collective-permute-done.10.refs_5_ = f32[4,64,128]{2,1,0:T(8,128)S(1)} collective-permute-done((f32[4,64,128]{2,1,0:T(8,128)}, f32[4,64,128]{2,1,0:T(8,128)S(1)}, u32[]{:S(2)}, u32[]{:S(2)}) %collective-permute-start.10) | collective-permute-done | bytes 131104 | tf_op jit(solution)/shard_map/ppermute | solution.py:352
  131.2 3.6 %collective-permute-done.11.refs_6_ = f32[4,64,128]{2,1,0:T(8,128)S(1)} collective-permute-done((f32[4,64,128]{2,1,0:T(8,128)}, f32[4,64,128]{2,1,0:T(8,128)S(1)}, u32[]{:S(2)}, u32[]{:S(2)}) %collective-permute-start.11) | collective-permute-done | bytes 131104 | tf_op jit(solution)/shard_map/ppermute | solution.py:353
  135.8 5.6 %wave_step.10 = (f32[4,64,32,128]{3,2,1,0:T(8,128)}, f32[32,32,128]{2,1,0:T(8,128)}, f32[32,32,128]{2,1,0:T(8,128)}, f32[4,64,128]{2,1,0:T(8,128)}, f32[4,64,128...) custom-call(f32[4,64,32,128]{3,2,1,0:T(8,128)} %get-tuple-element.48.refs_0_.refs_1_, ...), custom_call_target="tpu_custom_call" | custom-call | flops 20971520 | bytes 8388608 | tf_op jit(solution)/shard_map/wave_step/pallas_call | solution.py:209
  147.2 5.5 %wave_step.11 = (f32[4,64,32,128]{3,2,1,0:T(8,128)}, f32[32,32,128]{2,1,0:T(8,128)}, f32[32,32,128]{2,1,0:T(8,128)}, f32[4,64,128]{2,1,0:T(8,128)}, f32[4,64,128]{2,1,0:T(8,128)}) custom-call(f32[4,64,32,128]{3,2,1,0:T(8,128)} %get-tuple-element.48.refs_0_.refs_1_, ...), custom_call_target="tpu_custom_call", output_to_operand_aliasing={{0}: (7, {}), {3}: (8, {}), {4}: (9, {})} | custom-call | flops 20971520 | bytes 8388608 | tf_op jit(solution)/shard_map/wave_step/pallas_call | solution.py:209
  158.3 30.3 %collective-permute-done.20.refs_7_ = f32[4,1,32,128]{3,2,1,0:T(8,128)S(1)} collective-permute-done((f32[4,1,32,128]{3,2,1,0:T(8,128)S(1)}, f32[4,1,32,128]{3,2,1,0:T(8,128)S(1)}, u32[]{:S(2)}, u32[]{:S(2)}) %collective-permute-start.20) | collective-permute-done | bytes 65568 | tf_op jit(solution)/shard_map/ppermute | solution.py:347
  188.5 4.4 %collective-permute-start.21 = (f32[4,1,32,128]{3,2,1,0:T(8,128)S(1)}, f32[4,1,32,128]{3,2,1,0:T(8,128)S(1)}, u32[]{:S(2)}, u32[]{:S(2)}) collective-permute-start(f32[4,1,32,128]{3,2,1,0:T(8,128)S(1)} %copy-done.53), channel_id=1, source_target_pairs={{0,12},{4,0},{8,4},{12,8},{1,13},{5,1},{9,5},{13,9},{2,14},{6,2},{... | collective-permute-start | bytes 196616 | tf_op jit(solution)/shard_map/ppermute | solution.py:348
  193.0 4.0 %collective-permute-done.21.refs_8_ = f32[4,1,32,128]{3,2,1,0:T(8,128)S(1)} collective-permute-done((f32[4,1,32,128]{3,2,1,0:T(8,128)S(1)}, f32[4,1,32,128]{3,2,1,0:T(8,128)S(1)}, u32[]{:S(2)}, u32[]{:S(2)}) %collective-permute-start.21) | collective-permute-done | bytes 65568 | tf_op jit(solution)/shard_map/ppermute | solution.py:348
  196.9 5.3 %collective-permute-done.18.refs_5_ = f32[4,64,128]{2,1,0:T(8,128)S(1)} collective-permute-done((f32[4,64,128]{2,1,0:T(8,128)}, f32[4,64,128]{2,1,0:T(8,128)S(1)}, u32[]{:S(2)}, u32[]{:S(2)}) %collective-permute-start.18) | collective-permute-done | bytes 131104 | tf_op jit(solution)/shard_map/ppermute | solution.py:352
  202.2 5.3 %collective-permute-done.19.refs_6_ = f32[4,64,128]{2,1,0:T(8,128)S(1)} collective-permute-done((f32[4,64,128]{2,1,0:T(8,128)}, f32[4,64,128]{2,1,0:T(8,128)S(1)}, u32[]{:S(2)}, u32[]{:S(2)}) %collective-permute-start.19) | collective-permute-done | bytes 131104 | tf_op jit(solution)/shard_map/ppermute | solution.py:353
  208.5 5.6 %wave_step.12 = (f32[4,64,32,128]{3,2,1,0:T(8,128)}, f32[32,32,128]{2,1,0:T(8,128)}, f32[32,32,128]{2,1,0:T(8,128)}, f32[4,64,128]{2,1,0:T(8,128)}, f32[4,64,128...) custom-call(f32[4,64,32,128]{3,2,1,0:T(8,128)} %get-tuple-element.60.refs_, ...), custom_call_target="tpu_custom_call", output_to_operand_aliasing={{0}: (1, {})} | custom-call | flops 20971520 | bytes 8388608 | tf_op jit(solution)/shard_map/wave_step/pallas_call | solution.py:209
  214.1 3.5 %collective-permute-start.24 = (f32[32,32,128]{2,1,0:T(8,128)}, f32[32,32,128]{2,1,0:T(8,128)S(1)}, u32[]{:S(2)}, u32[]{:S(2)}) collective-permute-start(f32[32,32,128]{2,1,0:T(8,128)} %get-tuple-element.73), channel_id=1, source_target_pairs={{0,16},{16,32},{32,48},{48,0},{1,17},{17,33},{33,49},{49,1},{2,18}... | collective-permute-start | bytes 1572872 | tf_op jit(solution)/shard_map/ppermute | solution.py:342
  218.6 5.5 %wave_step.13 = (f32[4,64,32,128]{3,2,1,0:T(8,128)}, f32[32,32,128]{2,1,0:T(8,128)}, f32[32,32,128]{2,1,0:T(8,128)}, f32[4,64,128]{2,1,0:T(8,128)}, f32[4,64,128]{2,1,0:T(8,128)}) custom-call(f32[4,64,32,128]{3,2,1,0:T(8,128)} %get-tuple-element.60.refs_0_.refs_1_, ...), custom_call_target="tpu_custom_call", output_to_operand_aliasing={{0}: (1, {}), {3}: (7, {}), {4}: (8, {})} | custom-call | flops 20971520 | bytes 8388608 | tf_op jit(solution)/shard_map/wave_step/pallas_call | solution.py:209
  227.4 4.5 %collective-permute-start.28 = (f32[4,1,32,128]{3,2,1,0:T(8,128)S(1)}, f32[4,1,32,128]{3,2,1,0:T(8,128)S(1)}, u32[]{:S(2)}, u32[]{:S(2)}) collective-permute-start(f32[4,1,32,128]{3,2,1,0:T(8,128)S(1)} %copy-done.54), channel_id=1, source_target_pairs={{0,4},{4,8},{8,12},{12,0},{1,5},{5,9},{9,13},{13,1},{2,6},{6,10},{... | collective-permute-start | bytes 196616 | tf_op jit(solution)/shard_map/ppermute | solution.py:347
  232.0 32.6 %collective-permute-done.28.refs_7_ = f32[4,1,32,128]{3,2,1,0:T(8,128)S(1)} collective-permute-done((f32[4,1,32,128]{3,2,1,0:T(8,128)S(1)}, f32[4,1,32,128]{3,2,1,0:T(8,128)S(1)}, u32[]{:S(2)}, u32[]{:S(2)}) %collective-permute-start.28) | collective-permute-done | bytes 65568 | tf_op jit(solution)/shard_map/ppermute | solution.py:347
  264.5 5.3 %collective-permute-start.29 = (f32[4,1,32,128]{3,2,1,0:T(8,128)S(1)}, f32[4,1,32,128]{3,2,1,0:T(8,128)S(1)}, u32[]{:S(2)}, u32[]{:S(2)}) collective-permute-start(f32[4,1,32,128]{3,2,1,0:T(8,128)S(1)} %copy-done.51), channel_id=1, source_target_pairs={{0,12},{4,0},{8,4},{12,8},{1,13},{5,1},{9,5},{13,9},{2,14},{6,2},{... | collective-permute-start | bytes 196616 | tf_op jit(solution)/shard_map/ppermute | solution.py:348
  272.9 5.9 %collective-permute-done.26.refs_5_ = f32[4,64,128]{2,1,0:T(8,128)S(1)} collective-permute-done((f32[4,64,128]{2,1,0:T(8,128)}, f32[4,64,128]{2,1,0:T(8,128)S(1)}, u32[]{:S(2)}, u32[]{:S(2)}) %collective-permute-start.26) | collective-permute-done | bytes 131104 | tf_op jit(solution)/shard_map/ppermute | solution.py:352
  279.1 5.1 %collective-permute-done.27.refs_6_ = f32[4,64,128]{2,1,0:T(8,128)S(1)} collective-permute-done((f32[4,64,128]{2,1,0:T(8,128)}, f32[4,64,128]{2,1,0:T(8,128)S(1)}, u32[]{:S(2)}, u32[]{:S(2)}) %collective-permute-start.27) | collective-permute-done | bytes 131104 | tf_op jit(solution)/shard_map/ppermute | solution.py:353
  285.2 5.4 %wave_step.14 = (f32[4,64,32,128]{3,2,1,0:T(8,128)}, f32[16,32,128]{2,1,0:T(8,128)}, f32[16,32,128]{2,1,0:T(8,128)}) custom-call(f32[4,64,32,128]{3,2,1,0:T(8,128)} %get-tuple-element.72.refs_0_, f32[4,64,32,128]{3,2,1,0:T(8,128)} %get-tuple-element.60.refs_0_.refs_1_, f32[4,64,32,128]{3,2,1,0:T(8,128)} %refs_2_.15, ...), custom_call_target="tpu_custom_call", output_to_operand_aliasing={{0}: (1, {})} | custom-call | flops 20971520 | bytes 8388608 | tf_op jit(solution)/shard_map/wave_step/pallas_call | solution.py:209
  294.0 5.3 %wave_step.15 = (f32[4,64,32,128]{3,2,1,0:T(8,128)}, f32[16,32,128]{2,1,0:T(8,128)}, f32[8,32,128]{2,1,0:T(8,128)}, f32[8,32,128]{2,1,0:T(8,128)}) custom-call(f32[4,64,32,128]{3,2,1,0:T(8,128)} %get-tuple-element.72.refs_0_, f32[4,64,32,128]{3,2,1,0:T(8,128)} %get-tuple-element.79.refs_1_, ...), custom_call_target="tpu_custom_call", output_to_operand_aliasing={{0}: (1, {})} | custom-call | flops 20971520 | bytes 8388608 | tf_op jit(solution)/shard_map/wave_step/pallas_call | solution.py:209
  303.6 4.9 %collective-permute-done.32.refs_0_ = f32[16,32,128]{2,1,0:T(8,128)S(1)} collective-permute-done((f32[16,32,128]{2,1,0:T(8,128)}, f32[16,32,128]{2,1,0:T(8,128)S(1)}, u32[]{:S(2)}, u32[]{:S(2)}) %collective-permute-start.32) | collective-permute-done | bytes 262176 | tf_op jit(solution)/shard_map/ppermute | solution.py:411
  310.3 4.6 %collective-permute-start.35 = (f32[8,32,128]{2,1,0:T(8,128)}, f32[8,32,128]{2,1,0:T(8,128)S(1)}, u32[]{:S(2)}, u32[]{:S(2)}) collective-permute-start(f32[8,32,128]{2,1,0:T(8,128)} %get-tuple-element.84), channel_id=1, source_target_pairs={{0,16},{1,17},{2,18},{3,19},{4,20},{5,21},{6,22},{7,23},{8,24},{9,... | collective-permute-start | bytes 393224 | tf_op jit(solution)/shard_map/ppermute | solution.py:411
  323.9 3.3 %running_sums.2.refs_9_ = f32[4,64,32,128]{3,2,1,0:T(8,128)} custom-call(f32[4,64,32,128]{3,2,1,0:T(8,128)} %get-tuple-element.44.p_hbm, f32[16,32,128]{2,1,0:T(8,128)} %copy-done.2, f32[16,32,128]{2,1,0:T(8,128)} %copy-done.4, f32[16,32,128]{2,1,0:T(8,128)} %copy-done.39, f32[16,32,128]{2,1,0:T(8,128)} %copy-done.3, f32[16,32,128]{2,1,0:T(8,128)} %copy-done.5, ...), custom_call_target="tpu_custom_call" | custom-call | flops 5242880 | bytes 4194304 | tf_op jit(solution)/shard_map/running_sums/pallas_call | solution.py:303
  328.7 3.4 %running_sums.3 = f32[4,64,32,128]{3,2,1,0:T(8,128)} custom-call(f32[4,64,32,128]{3,2,1,0:T(8,128)} %get-tuple-element.44.p_hbm, f32[16,32,128]{2,1,0:T(8,128)} %copy-done, f32[16,32,128]{2,1,0:T(8,128)} %copy-done.1, f32[16,32,128]{2,1,0:T(8,128)} %copy-done.38, f32[8,32,128]{2,1,0:T(8,128)} %copy-done.19, ...), custom_call_target="tpu_custom_call", output_to_operand_aliasing={{}: (10, {})} | custom-call | flops 5242880 | bytes 4194304 | tf_op jit(solution)/shard_map/running_sums/pallas_call | solution.py:303
  (208 shorter events, 67.4 us)
Async XLA Ops:
  1.5 12.7 %collective-permute-start.7 = (f32[4,1,32,128]{3,2,1,0:T(8,128)S(1)}, f32[4,1,32,128]{3,2,1,0:T(8,128)S(1)}, u32[]{:S(2)}, u32[]{:S(2)}) collective-permute-start(f32[4,1,32,128]{3,2,1,0:T(8,128)S(1)} %get-tuple-element.88), channel_id=1, source_target_pairs={{0,12},{4,0},{8,4},{12,8},{1,13},{5,1},{9,5},{13,9},{2,14},{6,2},{... | collective-permute-start | bytes 196616 | tf_op jit(solution)/shard_map/ppermute | solution.py:348
  6.1 54.0 %collective-permute-start.4 = (f32[32,32,128]{2,1,0:T(8,128)S(1)}, f32[32,32,128]{2,1,0:T(8,128)S(1)}, u32[]{:S(2)}, u32[]{:S(2)}) collective-permute-start(f32[32,32,128]{2,1,0:T(8,128)S(1)} %pad_maximum_fusion), channel_id=1, source_target_pairs={{0,16},{16,32},{32,48},{48,0},{1,17},{17,33},{33,49},{49,1},{2,18}... | collective-permute-start | bytes 1572872 | tf_op jit(solution)/shard_map/ppermute | solution.py:342
  6.3 53.9 %collective-permute-start.5 = (f32[32,32,128]{2,1,0:T(8,128)S(1)}, f32[32,32,128]{2,1,0:T(8,128)S(1)}, u32[]{:S(2)}, u32[]{:S(2)}) collective-permute-start(f32[32,32,128]{2,1,0:T(8,128)S(1)} %pad_maximum_fusion.1), channel_id=1, source_target_pairs={{0,48},{16,0},{32,16},{48,32},{1,49},{17,1},{33,17},{49,33},{2,50}... | collective-permute-start | bytes 1572872 | tf_op jit(solution)/shard_map/ppermute | solution.py:342
  10.9 60.4 %collective-permute-start.1 = (f32[32,32,128]{2,1,0:T(8,128)S(1)}, f32[32,32,128]{2,1,0:T(8,128)S(1)}, u32[]{:S(2)}, u32[]{:S(2)}) collective-permute-start(f32[32,32,128]{2,1,0:T(8,128)S(1)} %get-tuple-element.96), channel_id=1, source_target_pairs={{0,48},{16,0},{32,16},{48,32},{1,49},{17,1},{33,17},{49,33},{2,50}... | collective-permute-start | bytes 1572872 | tf_op jit(solution)/shard_map/ppermute | solution.py:342
  11.8 59.5 %collective-permute-start = (f32[32,32,128]{2,1,0:T(8,128)S(1)}, f32[32,32,128]{2,1,0:T(8,128)S(1)}, u32[]{:S(2)}, u32[]{:S(2)}) collective-permute-start(f32[32,32,128]{2,1,0:T(8,128)S(1)} %get-tuple-element.97), channel_id=1, source_target_pairs={{0,16},{16,32},{32,48},{48,0},{1,17},{17,33},{33,49},{49,1},{2,18}... | collective-permute-start | bytes 1572872 | tf_op jit(solution)/shard_map/ppermute | solution.py:342
  14.2 35.6 %collective-permute-start.6 = (f32[4,1,32,128]{3,2,1,0:T(8,128)S(1)}, f32[4,1,32,128]{3,2,1,0:T(8,128)S(1)}, u32[]{:S(2)}, u32[]{:S(2)}) collective-permute-start(f32[4,1,32,128]{3,2,1,0:T(8,128)S(1)} %get-tuple-element.89), channel_id=1, source_target_pairs={{0,4},{4,8},{8,12},{12,0},{1,5},{5,9},{9,13},{13,1},{2,6},{6,10},{... | collective-permute-start | bytes 196616 | tf_op jit(solution)/shard_map/ppermute | solution.py:347
  67.4 67.4 %collective-permute-start.12 = (f32[32,32,128]{2,1,0:T(8,128)}, f32[32,32,128]{2,1,0:T(8,128)S(1)}, u32[]{:S(2)}, u32[]{:S(2)}) collective-permute-start(f32[32,32,128]{2,1,0:T(8,128)} %get-tuple-element.53), channel_id=1, source_target_pairs={{0,16},{16,32},{32,48},{48,0},{1,17},{17,33},{33,49},{49,1},{2,18}... | collective-permute-start | bytes 1572872 | tf_op jit(solution)/shard_map/ppermute | solution.py:342
  67.5 67.3 %collective-permute-start.13 = (f32[32,32,128]{2,1,0:T(8,128)}, f32[32,32,128]{2,1,0:T(8,128)S(1)}, u32[]{:S(2)}, u32[]{:S(2)}) collective-permute-start(f32[32,32,128]{2,1,0:T(8,128)} %get-tuple-element.54), channel_id=1, source_target_pairs={{0,48},{16,0},{32,16},{48,32},{1,49},{17,1},{33,17},{49,33},{2,50}... | collective-permute-start | bytes 1572872 | tf_op jit(solution)/shard_map/ppermute | solution.py:342
  77.7 68.5 %collective-permute-start.8 = (f32[32,32,128]{2,1,0:T(8,128)}, f32[32,32,128]{2,1,0:T(8,128)S(1)}, u32[]{:S(2)}, u32[]{:S(2)}) collective-permute-start(f32[32,32,128]{2,1,0:T(8,128)} %get-tuple-element.49), channel_id=1, source_target_pairs={{0,16},{16,32},{32,48},{48,0},{1,17},{17,33},{33,49},{49,1},{2,18}... | collective-permute-start | bytes 1572872 | tf_op jit(solution)/shard_map/ppermute | solution.py:342
  79.2 67.0 %collective-permute-start.9 = (f32[32,32,128]{2,1,0:T(8,128)}, f32[32,32,128]{2,1,0:T(8,128)S(1)}, u32[]{:S(2)}, u32[]{:S(2)}) collective-permute-start(f32[32,32,128]{2,1,0:T(8,128)} %get-tuple-element.50), channel_id=1, source_target_pairs={{0,48},{16,0},{32,16},{48,32},{1,49},{17,1},{33,17},{49,33},{2,50}... | collective-permute-start | bytes 1572872 | tf_op jit(solution)/shard_map/ppermute | solution.py:342
  81.1 21.6 %collective-permute-start.14 = (f32[4,1,32,128]{3,2,1,0:T(8,128)S(1)}, f32[4,1,32,128]{3,2,1,0:T(8,128)S(1)}, u32[]{:S(2)}, u32[]{:S(2)}) collective-permute-start(f32[4,1,32,128]{3,2,1,0:T(8,128)S(1)} %copy-done.55), channel_id=1, source_target_pairs={{0,4},{4,8},{8,12},{12,0},{1,5},{5,9},{9,13},{13,1},{2,6},{6,10},{... | collective-permute-start | bytes 196616 | tf_op jit(solution)/shard_map/ppermute | solution.py:347
  102.7 22.9 %collective-permute-start.15 = (f32[4,1,32,128]{3,2,1,0:T(8,128)S(1)}, f32[4,1,32,128]{3,2,1,0:T(8,128)S(1)}, u32[]{:S(2)}, u32[]{:S(2)}) collective-permute-start(f32[4,1,32,128]{3,2,1,0:T(8,128)S(1)} %copy-done.52), channel_id=1, source_target_pairs={{0,12},{4,0},{8,4},{12,8},{1,13},{5,1},{9,5},{13,9},{2,14},{6,2},{... | collective-permute-start | bytes 196616 | tf_op jit(solution)/shard_map/ppermute | solution.py:348
  141.4 66.1 %collective-permute-start.16 = (f32[32,32,128]{2,1,0:T(8,128)}, f32[32,32,128]{2,1,0:T(8,128)S(1)}, u32[]{:S(2)}, u32[]{:S(2)}) collective-permute-start(f32[32,32,128]{2,1,0:T(8,128)} %get-tuple-element.61), channel_id=1, source_target_pairs={{0,16},{16,32},{32,48},{48,0},{1,17},{17,33},{33,49},{49,1},{2,18}... | collective-permute-start | bytes 1572872 | tf_op jit(solution)/shard_map/ppermute | solution.py:342
  143.6 63.9 %collective-permute-start.17 = (f32[32,32,128]{2,1,0:T(8,128)}, f32[32,32,128]{2,1,0:T(8,128)S(1)}, u32[]{:S(2)}, u32[]{:S(2)}) collective-permute-start(f32[32,32,128]{2,1,0:T(8,128)} %get-tuple-element.62), channel_id=1, source_target_pairs={{0,48},{16,0},{32,16},{48,32},{1,49},{17,1},{33,17},{49,33},{2,50}... | collective-permute-start | bytes 1572872 | tf_op jit(solution)/shard_map/ppermute | solution.py:342
  152.7 64.9 %collective-permute-start.22 = (f32[32,32,128]{2,1,0:T(8,128)}, f32[32,32,128]{2,1,0:T(8,128)S(1)}, u32[]{:S(2)}, u32[]{:S(2)}) collective-permute-start(f32[32,32,128]{2,1,0:T(8,128)} %get-tuple-element.68), channel_id=1, source_target_pairs={{0,16},{16,32},{32,48},{48,0},{1,17},{17,33},{33,49},{49,1},{2,18}... | collective-permute-start | bytes 1572872 | tf_op jit(solution)/shard_map/ppermute | solution.py:342
  153.6 64.0 %collective-permute-start.23 = (f32[32,32,128]{2,1,0:T(8,128)}, f32[32,32,128]{2,1,0:T(8,128)S(1)}, u32[]{:S(2)}, u32[]{:S(2)}) collective-permute-start(f32[32,32,128]{2,1,0:T(8,128)} %get-tuple-element.69), channel_id=1, source_target_pairs={{0,48},{16,0},{32,16},{48,32},{1,49},{17,1},{33,17},{49,33},{2,50}... | collective-permute-start | bytes 1572872 | tf_op jit(solution)/shard_map/ppermute | solution.py:342
  156.0 32.5 %collective-permute-start.20 = (f32[4,1,32,128]{3,2,1,0:T(8,128)S(1)}, f32[4,1,32,128]{3,2,1,0:T(8,128)S(1)}, u32[]{:S(2)}, u32[]{:S(2)}) collective-permute-start(f32[4,1,32,128]{3,2,1,0:T(8,128)S(1)} %copy-done.56), channel_id=1, source_target_pairs={{0,4},{4,8},{8,12},{12,0},{1,5},{5,9},{9,13},{13,1},{2,6},{6,10},{... | collective-permute-start | bytes 196616 | tf_op jit(solution)/shard_map/ppermute | solution.py:347
  188.5 8.4 %collective-permute-start.21 = (f32[4,1,32,128]{3,2,1,0:T(8,128)S(1)}, f32[4,1,32,128]{3,2,1,0:T(8,128)S(1)}, u32[]{:S(2)}, u32[]{:S(2)}) collective-permute-start(f32[4,1,32,128]{3,2,1,0:T(8,128)S(1)} %copy-done.53), channel_id=1, source_target_pairs={{0,12},{4,0},{8,4},{12,8},{1,13},{5,1},{9,5},{13,9},{2,14},{6,2},{... | collective-permute-start | bytes 196616 | tf_op jit(solution)/shard_map/ppermute | solution.py:348
  214.1 70.0 %collective-permute-start.24 = (f32[32,32,128]{2,1,0:T(8,128)}, f32[32,32,128]{2,1,0:T(8,128)S(1)}, u32[]{:S(2)}, u32[]{:S(2)}) collective-permute-start(f32[32,32,128]{2,1,0:T(8,128)} %get-tuple-element.73), channel_id=1, source_target_pairs={{0,16},{16,32},{32,48},{48,0},{1,17},{17,33},{33,49},{49,1},{2,18}... | collective-permute-start | bytes 1572872 | tf_op jit(solution)/shard_map/ppermute | solution.py:342
  217.6 66.6 %collective-permute-start.25 = (f32[32,32,128]{2,1,0:T(8,128)}, f32[32,32,128]{2,1,0:T(8,128)S(1)}, u32[]{:S(2)}, u32[]{:S(2)}) collective-permute-start(f32[32,32,128]{2,1,0:T(8,128)} %get-tuple-element.74), channel_id=1, source_target_pairs={{0,48},{16,0},{32,16},{48,32},{1,49},{17,1},{33,17},{49,33},{2,50}... | collective-permute-start | bytes 1572872 | tf_op jit(solution)/shard_map/ppermute | solution.py:342
  224.1 69.1 %collective-permute-start.30 = (f32[32,32,128]{2,1,0:T(8,128)}, f32[32,32,128]{2,1,0:T(8,128)S(1)}, u32[]{:S(2)}, u32[]{:S(2)}) collective-permute-start(f32[32,32,128]{2,1,0:T(8,128)} %get-tuple-element.80), channel_id=1, source_target_pairs={{0,16},{16,32},{32,48},{48,0},{1,17},{17,33},{33,49},{49,1},{2,18}... | collective-permute-start | bytes 1572872 | tf_op jit(solution)/shard_map/ppermute | solution.py:342
  225.6 67.6 %collective-permute-start.31 = (f32[32,32,128]{2,1,0:T(8,128)}, f32[32,32,128]{2,1,0:T(8,128)}, u32[]{:S(2)}, u32[]{:S(2)}) collective-permute-start(f32[32,32,128]{2,1,0:T(8,128)} %get-tuple-element.81), channel_id=1, source_target_pairs={{0,48},{16,0},{32,16},{48,32},{1,49},{17,1},{33,17},{49,33},{2,50}... | collective-permute-start | bytes 1572872 | tf_op jit(solution)/shard_map/ppermute | solution.py:342
  227.4 37.1 %collective-permute-start.28 = (f32[4,1,32,128]{3,2,1,0:T(8,128)S(1)}, f32[4,1,32,128]{3,2,1,0:T(8,128)S(1)}, u32[]{:S(2)}, u32[]{:S(2)}) collective-permute-start(f32[4,1,32,128]{3,2,1,0:T(8,128)S(1)} %copy-done.54), channel_id=1, source_target_pairs={{0,4},{4,8},{8,12},{12,0},{1,5},{5,9},{9,13},{13,1},{2,6},{6,10},{... | collective-permute-start | bytes 196616 | tf_op jit(solution)/shard_map/ppermute | solution.py:347
  264.5 8.4 %collective-permute-start.29 = (f32[4,1,32,128]{3,2,1,0:T(8,128)S(1)}, f32[4,1,32,128]{3,2,1,0:T(8,128)S(1)}, u32[]{:S(2)}, u32[]{:S(2)}) collective-permute-start(f32[4,1,32,128]{3,2,1,0:T(8,128)S(1)} %copy-done.51), channel_id=1, source_target_pairs={{0,12},{4,0},{8,4},{12,8},{1,13},{5,1},{9,5},{13,9},{2,14},{6,2},{... | collective-permute-start | bytes 196616 | tf_op jit(solution)/shard_map/ppermute | solution.py:348
  290.6 10.3 %collective-permute-start.41 = (f32[16,32,128]{2,1,0:T(8,128)}, f32[16,32,128]{2,1,0:T(8,128)S(1)}, u32[]{:S(2)}, u32[]{:S(2)}) collective-permute-start(f32[16,32,128]{2,1,0:T(8,128)} %get-tuple-element.86), channel_id=1, source_target_pairs={{0,16},{1,17},{2,18},{3,19},{4,20},{5,21},{6,22},{7,23},{8,24},{9,... | collective-permute-start | bytes 786440 | tf_op jit(solution)/shard_map/ppermute | solution.py:411
  291.9 11.0 %collective-permute-start.44 = (f32[16,32,128]{2,1,0:T(8,128)}, f32[16,32,128]{2,1,0:T(8,128)S(1)}, u32[]{:S(2)}, u32[]{:S(2)}) collective-permute-start(f32[16,32,128]{2,1,0:T(8,128)} %get-tuple-element.87), channel_id=1, source_target_pairs={{0,16},{1,17},{2,18},{3,19},{4,20},{5,21},{6,22},{7,23},{8,24},{9,... | collective-permute-start | bytes 786440 | tf_op jit(solution)/shard_map/ppermute | solution.py:411
  299.4 9.1 %collective-permute-start.32 = (f32[16,32,128]{2,1,0:T(8,128)}, f32[16,32,128]{2,1,0:T(8,128)S(1)}, u32[]{:S(2)}, u32[]{:S(2)}) collective-permute-start(f32[16,32,128]{2,1,0:T(8,128)} %get-tuple-element.83), channel_id=1, source_target_pairs={{0,16},{1,17},{2,18},{3,19},{4,20},{5,21},{6,22},{7,23},{8,24},{9,... | collective-permute-start | bytes 786440 | tf_op jit(solution)/shard_map/ppermute | solution.py:411
  300.9 15.3 %collective-permute-start.42 = (f32[16,32,128]{2,1,0:T(8,128)S(1)}, f32[16,32,128]{2,1,0:T(8,128)S(1)}, u32[]{:S(2)}, u32[]{:S(2)}) collective-permute-start(f32[16,32,128]{2,1,0:T(8,128)S(1)} %add.36), channel_id=1, source_target_pairs={{16,32},{17,33},{18,34},{19,35},{20,36},{21,37},{22,38},{23,39},{2... | collective-permute-start | bytes 786440 | tf_op jit(solution)/shard_map/ppermute | solution.py:411
  302.9 14.0 %collective-permute-start.45 = (f32[16,32,128]{2,1,0:T(8,128)S(1)}, f32[16,32,128]{2,1,0:T(8,128)S(1)}, u32[]{:S(2)}, u32[]{:S(2)}) collective-permute-start(f32[16,32,128]{2,1,0:T(8,128)S(1)} %add.38), channel_id=1, source_target_pairs={{16,32},{17,33},{18,34},{19,35},{20,36},{21,37},{22,38},{23,39},{2... | collective-permute-start | bytes 786440 | tf_op jit(solution)/shard_map/ppermute | solution.py:411
  309.6 10.6 %collective-permute-start.33 = (f32[16,32,128]{2,1,0:T(8,128)S(1)}, f32[16,32,128]{2,1,0:T(8,128)S(1)}, u32[]{:S(2)}, u32[]{:S(2)}) collective-permute-start(f32[16,32,128]{2,1,0:T(8,128)S(1)} %add.30), channel_id=1, source_target_pairs={{16,32},{17,33},{18,34},{19,35},{20,36},{21,37},{22,38},{23,39},{2... | collective-permute-start | bytes 786440 | tf_op jit(solution)/shard_map/ppermute | solution.py:411
  310.3 7.5 %collective-permute-start.35 = (f32[8,32,128]{2,1,0:T(8,128)}, f32[8,32,128]{2,1,0:T(8,128)S(1)}, u32[]{:S(2)}, u32[]{:S(2)}) collective-permute-start(f32[8,32,128]{2,1,0:T(8,128)} %get-tuple-element.84), channel_id=1, source_target_pairs={{0,16},{1,17},{2,18},{3,19},{4,20},{5,21},{6,22},{7,23},{8,24},{9,... | collective-permute-start | bytes 393224 | tf_op jit(solution)/shard_map/ppermute | solution.py:411
  320.3 7.1 %collective-permute-start.34 = (f32[16,32,128]{2,1,0:T(8,128)S(1)}, f32[16,32,128]{2,1,0:T(8,128)S(1)}, u32[]{:S(2)}, u32[]{:S(2)}) collective-permute-start(f32[16,32,128]{2,1,0:T(8,128)S(1)} %add.31), channel_id=1, source_target_pairs={{32,48},{33,49},{34,50},{35,51},{36,52},{37,53},{38,54},{39,55},{4... | collective-permute-start | bytes 786440 | tf_op jit(solution)/shard_map/ppermute | solution.py:411
  (72 other events, 606.0 us)
where the time goes:
time: 338 us; the launch traced here: 332 us
  waiting for transfers between devices  154 us (46%)
  starting transfers between devices  107 us (32%)
  Pallas kernels  50.7 us (15%)
  local copies, waits for them, and re-layouts  15.6 us (5%)
    ppermute x4, waiting for transfers between devices, exchange(): lax.ppermute(ilast, 'cols', ring('cols', 1))  103 us
    pallas_call x8, Pallas kernels, step(): pl.pallas_call(body, out_shape=outs, in_specs=[hbm] * len(args), out_spec...  44 us
    ppermute x4, starting transfers between devices, exchange(): lax.ppermute(ifirst, 'cols', ring('cols', -1))  34.9 us
    ppermute x4, starting transfers between devices, exchange(): lax.ppermute(ilast, 'cols', ring('cols', 1))  24.3 us
    ppermute x4, waiting for transfers between devices, exchange(): lax.ppermute(klast, 'slabs', ring('slabs', 1))  21.5 us
    ppermute x8, starting transfers between devices, exchange(): lax.ppermute(dn, 'rows', ring('rows', -1))  16.7 us
    ppermute x15, starting transfers between devices, local(): got = lax.ppermute(carried, 'rows', [(s, s + 1)])  16.7 us
    ppermute x4, waiting for transfers between devices, exchange(): lax.ppermute(kfirst, 'slabs', ring('slabs', -1))  15.8 us
  transfers between devices with their start and end apart: 47, of which 18 were waited for; matrix products, arithmetic and copies ran while one was open for 2% of the time, Pallas kernels for 14%

commit v1 on v0

--- a/solution.py
+++ b/solution.py
@@ -11,7 +11,7 @@
 STEPS = 4
 GRID_J = 16
 WIDTHS = (32, 32)
-WRAP = 16
+FIRST = 16
 GROUP = 8
 PIECES = ((16, 16), (16, 8, 8))
 
@@ -333,22 +333,20 @@
 
 def local(pressure, earlier, speed_square):
     rows, total, depth, _ = pressure.shape
-    starts = [(total - WRAP + sum(WIDTHS[:a])) % total for a in range(len(WIDTHS))]
+    starts = [FIRST + sum(WIDTHS[:a]) for a in range(len(WIDTHS))]
     chunks = list(zip(starts, WIDTHS))
+    last = len(chunks) - 1
 
     def exchange(edges, a):
         dn, up, kfirst, klast = edges[:4]
         got = [
             lax.ppermute(up, "rows", ring("rows", 1)), lax.ppermute(dn, "rows", ring("rows", -1))
         ]
-        if a == 0:
+        if a == last:
             ifirst, ilast = edges[4:]
             got += [
                 lax.ppermute(ilast, "cols", ring("cols", 1)),
                 lax.ppermute(ifirst, "cols", ring("cols", -1)),
-            ]
-        if a == len(chunks) - 1:
-            got += [
                 lax.ppermute(klast, "slabs", ring("slabs", 1)),
                 lax.ppermute(kfirst, "slabs", ring("slabs", -1)),
             ]
@@ -371,7 +369,7 @@
 
         edges = [part(pressure[j], start, width, 0) for j in (0, rows - 1)]
         edges += [part(pressure[:, :, k], starts[0], total, 1) for k in (0, depth - 1)]
-        if a == 0:
+        if a == last:
             edges += [pressure[:, :1], pressure[:, total - 1 :]]
         return edges
 
@@ -383,7 +381,7 @@
         made, slabs = [], []
         for a, (start, width) in enumerate(chunks):
             before = older if t < 2 else fresh
-            halo = halos[a][:2] + halos[-1][-2:] + (halos[0][2:4] if a == 0 else [])
+            halo = halos[a][:2] + halos[last][4:] + (halos[last][2:4] if a == last else [])
             fresh, *edges = step(
                 newer,
                 before,

time: 338 us -> 256 us (0.76)
  waiting for transfers between devices: 154 us -> 98.1 us
  starting transfers between devices: 107 us -> 82.1 us
    ppermute x4, waiting for transfers between devices: 103 us -> 14.3 us  [exchange(): lax.ppermute(ilast, 'cols', ring('cols', 1))]
    ppermute x4, starting transfers between devices: 34.9 us -> 3.4 us  [exchange(): lax.ppermute(ifirst, 'cols', ring('cols', -1))]
    ppermute x4, waiting for transfers between devices: 7.98 us -> 29.7 us  [exchange(): lax.ppermute(ifirst, 'cols', ring('cols', -1))]
    ppermute x8, waiting for transfers between devices: 0.02 us -> 14.6 us  [exchange(): lax.ppermute(dn, 'rows', ring('rows', -1))]
    ppermute x8, starting transfers between devices: 10.3 us -> 4.3 us  [exchange(): lax.ppermute(up, 'rows', ring('rows', 1))]
    ppermute x4, waiting for transfers between devices: 21.5 us -> 16.4 us  [exchange(): lax.ppermute(klast, 'slabs', ring('slabs', 1))]
    ppermute x8, waiting for transfers between devices: 0.02 us -> 5.11 us  [exchange(): lax.ppermute(up, 'rows', ring('rows', 1))]
    ppermute x4, starting transfers between devices: 0.91 us -> 5.58 us  [exchange(): lax.ppermute(klast, 'slabs', ring('slabs', 1))]
  transfers between devices with their start and end apart: 47 -> 47, of which waited for: 18 -> 18; matrix products, arithmetic and copies ran while one was open for 2% -> 3% of each run, Pallas kernels for 14% -> 19%
where the time goes in v1:
time: 256 us; the launch traced here: 251 us
  waiting for transfers between devices  98.1 us (38%)
  starting transfers between devices  82.1 us (32%)
  Pallas kernels  50.7 us (20%)
  local copies, waits for them, and re-layouts  15.5 us (6%)
  other arithmetic  3.07 us (1%)
    pallas_call x8, Pallas kernels, step(): pl.pallas_call(body, out_shape=outs, in_specs=[hbm] * len(args), out_spec...  44 us
    ppermute x4, waiting for transfers between devices, exchange(): lax.ppermute(ifirst, 'cols', ring('cols', -1))  29.7 us
    ppermute x4, starting transfers between devices, exchange(): lax.ppermute(ilast, 'cols', ring('cols', 1))  22.3 us
    ppermute x8, starting transfers between devices, exchange(): lax.ppermute(dn, 'rows', ring('rows', -1))  20.1 us
    ppermute x15, starting transfers between devices, local(): got = lax.ppermute(carried, 'rows', [(s, s + 1)])  19.1 us
    ppermute x4, waiting for transfers between devices, exchange(): lax.ppermute(klast, 'slabs', ring('slabs', 1))  16.4 us
    ppermute x8, waiting for transfers between devices, exchange(): lax.ppermute(dn, 'rows', ring('rows', -1))  14.6 us
    ppermute x4, waiting for transfers between devices, exchange(): lax.ppermute(ilast, 'cols', ring('cols', 1))  14.3 us
  transfers between devices with their start and end apart: 47, of which 18 were waited for; matrix products, arithmetic and copies ran while one was open for 3% of the time, Pallas kernels for 19%

profile of v1, /device:TPU:1, one launch (start us, length us, event | category | flops | bytes accessed | tf_op | source)
XLA Modules:
  0.0 251.3 jit_solution(5319286256624657641)
XLA Ops:
  18.9 3.3 %collective-permute-done.2.refs_5_ = f32[4,64,128]{2,1,0:T(8,128)S(1)} collective-permute-done((f32[4,64,128]{2,1,0:T(8,128)S(1)}, f32[4,64,128]{2,1,0:T(8,128)S(1)}, u32[]{:S(2)}, u32[]{:S(2)}) %collective-permute-start.2) | collective-permute-done | bytes 131104 | tf_op jit(solution)/shard_map/ppermute | solution.py:350
  22.2 3.4 %collective-permute-start.5 = (f32[4,1,32,128]{3,2,1,0:T(8,128)}, f32[4,1,32,128]{3,2,1,0:T(8,128)S(1)}, u32[]{:S(2)}, u32[]{:S(2)}) collective-permute-start(f32[4,1,32,128]{3,2,1,0:T(8,128)} %get-tuple-element.90), channel_id=1, source_target_pairs={{0,12},{4,0},{8,4},{12,8},{1,13},{5,1},{9,5},{13,9},{2,14},{6,2},{... | collective-permute-start | bytes 196616 | tf_op jit(solution)/shard_map/ppermute | solution.py:349
  25.6 14.6 %collective-permute-done.7.refs_4_ = f32[32,32,128]{2,1,0:T(8,128)S(1)} collective-permute-done((f32[32,32,128]{2,1,0:T(8,128)S(1)}, f32[32,32,128]{2,1,0:T(8,128)S(1)}, u32[]{:S(2)}, u32[]{:S(2)}) %collective-permute-start.7) | collective-permute-done | bytes 524320 | tf_op jit(solution)/shard_map/ppermute | solution.py:343
  40.1 7.2 %collective-permute-start.4 = (f32[4,1,32,128]{3,2,1,0:T(8,128)}, f32[4,1,32,128]{3,2,1,0:T(8,128)S(1)}, u32[]{:S(2)}, u32[]{:S(2)}) collective-permute-start(f32[4,1,32,128]{3,2,1,0:T(8,128)} %get-tuple-element.91), channel_id=1, source_target_pairs={{0,4},{4,8},{8,12},{12,0},{1,5},{5,9},{9,13},{13,1},{2,6},{6,10},{... | collective-permute-start | bytes 196616 | tf_op jit(solution)/shard_map/ppermute | solution.py:348
  47.4 5.1 %collective-permute-done.6.refs_3_ = f32[32,32,128]{2,1,0:T(8,128)S(1)} collective-permute-done((f32[32,32,128]{2,1,0:T(8,128)S(1)}, f32[32,32,128]{2,1,0:T(8,128)S(1)}, u32[]{:S(2)}, u32[]{:S(2)}) %collective-permute-start.6) | collective-permute-done | bytes 524320 | tf_op jit(solution)/shard_map/ppermute | solution.py:343
  53.3 5.5 %wave_step.8 = (f32[4,64,32,128]{3,2,1,0:T(8,128)}, f32[32,32,128]{2,1,0:T(8,128)}, f32[32,32,128]{2,1,0:T(8,128)}, f32[4,64,128]{2,1,0:T(8,128)}, f32[4,64,128]{2,1,0:T(8,128)}) custom-call(f32[4,64,32,128]{3,2,1,0:T(8,128)} %refs_1_.7, f32[4,64,32,128]{3,2,1,0:T(8,128)} %refs_1_.5, f32[4,64,32,128]{3,2,1,0:T(8,128)} %refs_2_.15, ...), custom_call_target="tpu_custom_call" | custom-call | flops 20971520 | bytes 8388608 | tf_op jit(solution)/shard_map/wave_step/pallas_call | solution.py:209
  58.8 3.2 %collective-permute-start.15 = (f32[32,32,128]{2,1,0:T(8,128)}, f32[32,32,128]{2,1,0:T(8,128)S(1)}, u32[]{:S(2)}, u32[]{:S(2)}) collective-permute-start(f32[32,32,128]{2,1,0:T(8,128)} %get-tuple-element.56), channel_id=1, source_target_pairs={{0,48},{16,0},{32,16},{48,32},{1,49},{17,1},{33,17},{49,33},{2,50}... | collective-permute-start | bytes 1572872 | tf_op jit(solution)/shard_map/ppermute | solution.py:343
  63.1 5.6 %wave_step.9 = (f32[4,64,32,128]{3,2,1,0:T(8,128)}, f32[32,32,128]{2,1,0:T(8,128)}, f32[32,32,128]{2,1,0:T(8,128)}, f32[4,64,128]{2,1,0:T(8,128)}, f32[4,64,128]...) custom-call(f32[4,64,32,128]{3,2,1,0:T(8,128)} %refs_1_.7, ...), custom_call_target="tpu_custom_call", output_to_operand_aliasing={{0}: (9, {}), {3}: (10, {}), {4}: (11, {})} | custom-call | flops 20971520 | bytes 8388608 | tf_op jit(solution)/shard_map/wave_step/pallas_call | solution.py:209
  68.8 3.3 %collective-permute-start.9 = (f32[32,32,128]{2,1,0:T(8,128)}, f32[32,32,128]{2,1,0:T(8,128)S(1)}, u32[]{:S(2)}, u32[]{:S(2)}) collective-permute-start(f32[32,32,128]{2,1,0:T(8,128)} %get-tuple-element.50), channel_id=1, source_target_pairs={{0,48},{16,0},{32,16},{48,32},{1,49},{17,1},{33,17},{49,33},{2,50}... | collective-permute-start | bytes 1572872 | tf_op jit(solution)/shard_map/ppermute | solution.py:343
  74.1 3.9 %collective-permute-done.10.refs_5_ = f32[4,64,128]{2,1,0:T(8,128)S(1)} collective-permute-done((f32[4,64,128]{2,1,0:T(8,128)}, f32[4,64,128]{2,1,0:T(8,128)S(1)}, u32[]{:S(2)}, u32[]{:S(2)}) %collective-permute-start.10) | collective-permute-done | bytes 131104 | tf_op jit(solution)/shard_map/ppermute | solution.py:350
  82.4 10.9 %collective-permute-start.12 = (f32[4,1,32,128]{3,2,1,0:T(8,128)}, f32[4,1,32,128]{3,2,1,0:T(8,128)S(1)}, u32[]{:S(2)}, u32[]{:S(2)}) collective-permute-start(f32[4,1,32,128]{3,2,1,0:T(8,128)} %get-tuple-element.53), channel_id=1, source_target_pairs={{0,4},{4,8},{8,12},{12,0},{1,5},{5,9},{9,13},{13,1},{2,6},{6,10},{... | collective-permute-start | bytes 196616 | tf_op jit(solution)/shard_map/ppermute | solution.py:348
  94.3 5.5 %wave_step.10 = (f32[4,64,32,128]{3,2,1,0:T(8,128)}, f32[32,32,128]{2,1,0:T(8,128)}, f32[32,32,128]{2,1,0:T(8,128)}, f32[4,64,128]{2,1,0:T(8,128)}, f32[4,64,128]{2,1,0:T(8,128)}) custom-call(f32[4,64,32,128]{3,2,1,0:T(8,128)} %get-tuple-element.48.refs_0_.refs_1_, f32[4,64,32,128]{3,2,1,0:T(8,128)} %refs_1_.7, f32[4,64,32,128]{3,2,1,0:T(8,128)} %refs_2_.15, ...), custom_call_target="tpu_custom_call" | custom-call | flops 20971520 | bytes 8388608 | tf_op jit(solution)/shard_map/wave_step/pallas_call | solution.py:209
  99.9 4.5 %collective-permute-done.12.refs_7_ = f32[4,1,32,128]{3,2,1,0:T(8,128)S(1)} collective-permute-done((f32[4,1,32,128]{3,2,1,0:T(8,128)}, f32[4,1,32,128]{3,2,1,0:T(8,128)S(1)}, u32[]{:S(2)}, u32[]{:S(2)}) %collective-permute-start.12) | collective-permute-done | bytes 65568 | tf_op jit(solution)/shard_map/ppermute | solution.py:348
  106.1 10.6 %collective-permute-done.13.refs_8_ = f32[4,1,32,128]{3,2,1,0:T(8,128)S(1)} collective-permute-done((f32[4,1,32,128]{3,2,1,0:T(8,128)}, f32[4,1,32,128]{3,2,1,0:T(8,128)S(1)}, u32[]{:S(2)}, u32[]{:S(2)}) %collective-permute-start.13) | collective-permute-done | bytes 65568 | tf_op jit(solution)/shard_map/ppermute | solution.py:349
  117.7 5.6 %wave_step.11 = (f32[4,64,32,128]{3,2,1,0:T(8,128)}, f32[32,32,128]{2,1,0:T(8,128)}, f32[32,32,128]{2,1,0:T(8,128)}, f32[4,64,128]{2,1,0:T(8,128)}, f32[4,64,128...) custom-call(f32[4,64,32,128]{3,2,1,0:T(8,128)} %get-tuple-element.48, ...), custom_call_target="tpu_custom_call", output_to_operand_aliasing={{0}: (9, {}), {3}: (10, {}), {4}: (11, {})} | custom-call | flops 20971520 | bytes 8388608 | tf_op jit(solution)/shard_map/wave_step/pallas_call | solution.py:209
  128.2 4.6 %collective-permute-done.18.refs_5_ = f32[4,64,128]{2,1,0:T(8,128)S(1)} collective-permute-done((f32[4,64,128]{2,1,0:T(8,128)}, f32[4,64,128]{2,1,0:T(8,128)S(1)}, u32[]{:S(2)}, u32[]{:S(2)}) %collective-permute-start.18) | collective-permute-done | bytes 131104 | tf_op jit(solution)/shard_map/ppermute | solution.py:350
  134.4 3.7 %collective-permute-done.19.refs_6_ = f32[4,64,128]{2,1,0:T(8,128)S(1)} collective-permute-done((f32[4,64,128]{2,1,0:T(8,128)}, f32[4,64,128]{2,1,0:T(8,128)S(1)}, u32[]{:S(2)}, u32[]{:S(2)}) %collective-permute-start.19) | collective-permute-done | bytes 131104 | tf_op jit(solution)/shard_map/ppermute | solution.py:351
  141.4 5.5 %wave_step.12 = (f32[4,64,32,128]{3,2,1,0:T(8,128)}, f32[32,32,128]{2,1,0:T(8,128)}, f32[32,32,128]{2,1,0:T(8,128)}, f32[4,64,128]{2,1,0:T(8,128)}, f32[4,64,128]{2,1,0:T(8,128)}) custom-call(f32[4,64,32,128]{3,2,1,0:T(8,128)} %get-tuple-element.60.refs_0_.refs_1_, ...), custom_call_target="tpu_custom_call", output_to_operand_aliasing={{0}: (1, {})} | custom-call | flops 20971520 | bytes 8388608 | tf_op jit(solution)/shard_map/wave_step/pallas_call | solution.py:209
  146.9 5.1 %collective-permute-done.22.refs_7_ = f32[4,1,32,128]{3,2,1,0:T(8,128)S(1)} collective-permute-done((f32[4,1,32,128]{3,2,1,0:T(8,128)}, f32[4,1,32,128]{3,2,1,0:T(8,128)S(1)}, u32[]{:S(2)}, u32[]{:S(2)}) %collective-permute-start.22) | collective-permute-done | bytes 65568 | tf_op jit(solution)/shard_map/ppermute | solution.py:348
  153.8 10.6 %collective-permute-done.23.refs_8_ = f32[4,1,32,128]{3,2,1,0:T(8,128)S(1)} collective-permute-done((f32[4,1,32,128]{3,2,1,0:T(8,128)}, f32[4,1,32,128]{3,2,1,0:T(8,128)S(1)}, u32[]{:S(2)}, u32[]{:S(2)}) %collective-permute-start.23) | collective-permute-done | bytes 65568 | tf_op jit(solution)/shard_map/ppermute | solution.py:349
  165.5 5.6 %wave_step.13 = (f32[4,64,32,128]{3,2,1,0:T(8,128)}, f32[32,32,128]{2,1,0:T(8,128)}, f32[32,32,128]{2,1,0:T(8,128)}, f32[4,64,128]{2,1,0:T(8,128)}, f32[4,64,128...) custom-call(f32[4,64,32,128]{3,2,1,0:T(8,128)} %get-tuple-element.60, ...), custom_call_target="tpu_custom_call", output_to_operand_aliasing={{0}: (1, {}), {3}: (9, {}), {4}: (10, {})} | custom-call | flops 20971520 | bytes 8388608 | tf_op jit(solution)/shard_map/wave_step/pallas_call | solution.py:209
  176.0 4.6 %collective-permute-done.26.refs_5_ = f32[4,64,128]{2,1,0:T(8,128)S(1)} collective-permute-done((f32[4,64,128]{2,1,0:T(8,128)}, f32[4,64,128]{2,1,0:T(8,128)S(1)}, u32[]{:S(2)}, u32[]{:S(2)}) %collective-permute-start.26) | collective-permute-done | bytes 131104 | tf_op jit(solution)/shard_map/ppermute | solution.py:350
  182.2 3.8 %collective-permute-done.27.refs_6_ = f32[4,64,128]{2,1,0:T(8,128)S(1)} collective-permute-done((f32[4,64,128]{2,1,0:T(8,128)}, f32[4,64,128]{2,1,0:T(8,128)S(1)}, u32[]{:S(2)}, u32[]{:S(2)}) %collective-permute-start.27) | collective-permute-done | bytes 131104 | tf_op jit(solution)/shard_map/ppermute | solution.py:351
  188.8 5.3 %wave_step.14 = (f32[4,64,32,128]{3,2,1,0:T(8,128)}, f32[16,32,128]{2,1,0:T(8,128)}, f32[16,32,128]{2,1,0:T(8,128)}) custom-call(f32[4,64,32,128]{3,2,1,0:T(8,128)} %get-tuple-element.72.refs_0_, f32[4,64,32,128]{3,2,1,0:T(8,128)} %get-tuple-element.60.refs_0_.refs_1_, f32[4,64,32,128]{3,2,1,0:T(8,128)} %refs_2_.15, ...), custom_call_target="tpu_custom_call", output_to_operand_aliasing={{0}: (1, {})} | custom-call | flops 20971520 | bytes 8388608 | tf_op jit(solution)/shard_map/wave_step/pallas_call | solution.py:209
  195.5 4.6 %collective-permute-done.30.refs_7_ = f32[4,1,32,128]{3,2,1,0:T(8,128)S(1)} collective-permute-done((f32[4,1,32,128]{3,2,1,0:T(8,128)}, f32[4,1,32,128]{3,2,1,0:T(8,128)S(1)}, u32[]{:S(2)}, u32[]{:S(2)}) %collective-permute-start.30) | collective-permute-done | bytes 65568 | tf_op jit(solution)/shard_map/ppermute | solution.py:348
  200.1 3.7 %collective-permute-start.44 = (f32[16,32,128]{2,1,0:T(8,128)}, f32[16,32,128]{2,1,0:T(8,128)S(1)}, u32[]{:S(2)}, u32[]{:S(2)}) collective-permute-start(f32[16,32,128]{2,1,0:T(8,128)} %get-tuple-element.87), channel_id=1, source_target_pairs={{0,16},{1,17},{2,18},{3,19},{4,20},{5,21},{6,22},{7,23},{8,24},{9,... | collective-permute-start | bytes 786440 | tf_op jit(solution)/shard_map/ppermute | solution.py:409
  203.8 8.4 %collective-permute-done.31.refs_8_ = f32[4,1,32,128]{3,2,1,0:T(8,128)S(1)} collective-permute-done((f32[4,1,32,128]{3,2,1,0:T(8,128)}, f32[4,1,32,128]{3,2,1,0:T(8,128)S(1)}, u32[]{:S(2)}, u32[]{:S(2)}) %collective-permute-start.31) | collective-permute-done | bytes 65568 | tf_op jit(solution)/shard_map/ppermute | solution.py:349
  213.3 5.4 %wave_step.15 = (f32[4,64,32,128]{3,2,1,0:T(8,128)}, f32[16,32,128]{2,1,0:T(8,128)}, f32[8,32,128]{2,1,0:T(8,128)}, f32[8,32,128]{2,1,0:T(8,128)}) custom-call(f32[4,64,32,128]{3,2,1,0:T(8,128)} %get-tuple-element.72.refs_0_, f32[4,64,32,128]{3,2,1,0:T(8,128)} %get-tuple-element.77.refs_1_, ...), custom_call_target="tpu_custom_call", output_to_operand_aliasing={{0}: (1, {})} | custom-call | flops 20971520 | bytes 8388608 | tf_op jit(solution)/shard_map/wave_step/pallas_call | solution.py:209
  221.7 4.9 %collective-permute-done.32.refs_0_ = f32[16,32,128]{2,1,0:T(8,128)S(1)} collective-permute-done((f32[16,32,128]{2,1,0:T(8,128)}, f32[16,32,128]{2,1,0:T(8,128)S(1)}, u32[]{:S(2)}, u32[]{:S(2)}) %collective-permute-start.32) | collective-permute-done | bytes 262176 | tf_op jit(solution)/shard_map/ppermute | solution.py:409
  228.3 4.6 %collective-permute-start.35 = (f32[8,32,128]{2,1,0:T(8,128)}, f32[8,32,128]{2,1,0:T(8,128)S(1)}, u32[]{:S(2)}, u32[]{:S(2)}) collective-permute-start(f32[8,32,128]{2,1,0:T(8,128)} %get-tuple-element.84), channel_id=1, source_target_pairs={{0,16},{1,17},{2,18},{3,19},{4,20},{5,21},{6,22},{7,23},{8,24},{9,... | collective-permute-start | bytes 393224 | tf_op jit(solution)/shard_map/ppermute | solution.py:409
  242.9 3.3 %running_sums.2.refs_9_ = f32[4,64,32,128]{3,2,1,0:T(8,128)} custom-call(f32[4,64,32,128]{3,2,1,0:T(8,128)} %get-tuple-element.44.p_hbm, f32[16,32,128]{2,1,0:T(8,128)} %copy-done.2, f32[16,32,128]{2,1,0:T(8,128)} %copy-done.4, f32[16,32,128]{2,1,0:T(8,128)} %copy-done.40, f32[16,32,128]{2,1,0:T(8,128)} %copy-done.3, f32[16,32,128]{2,1,0:T(8,128)} %copy-done.5, ...), custom_call_target="tpu_custom_call" | custom-call | flops 5242880 | bytes 4194304 | tf_op jit(solution)/shard_map/running_sums/pallas_call | solution.py:303
  247.7 3.4 %running_sums.3 = f32[4,64,32,128]{3,2,1,0:T(8,128)} custom-call(f32[4,64,32,128]{3,2,1,0:T(8,128)} %get-tuple-element.44.p_hbm, f32[16,32,128]{2,1,0:T(8,128)} %copy-done, f32[16,32,128]{2,1,0:T(8,128)} %copy-done.1, f32[16,32,128]{2,1,0:T(8,128)} %copy-done.39, f32[8,32,128]{2,1,0:T(8,128)} %copy-done.19, ...), custom_call_target="tpu_custom_call", output_to_operand_aliasing={{}: (10, {})} | custom-call | flops 5242880 | bytes 4194304 | tf_op jit(solution)/shard_map/running_sums/pallas_call | solution.py:303
  (198 shorter events, 70.0 us)
Async XLA Ops:
  1.9 60.1 %collective-permute-start = (f32[32,32,128]{2,1,0:T(8,128)S(1)}, f32[32,32,128]{2,1,0:T(8,128)S(1)}, u32[]{:S(2)}, u32[]{:S(2)}) collective-permute-start(f32[32,32,128]{2,1,0:T(8,128)S(1)} %pad_maximum_fusion), channel_id=1, source_target_pairs={{0,16},{16,32},{32,48},{48,0},{1,17},{17,33},{33,49},{49,1},{2,18}... | collective-permute-start | bytes 1572872 | tf_op jit(solution)/shard_map/ppermute | solution.py:343
  4.5 57.6 %collective-permute-start.1 = (f32[32,32,128]{2,1,0:T(8,128)S(1)}, f32[32,32,128]{2,1,0:T(8,128)S(1)}, u32[]{:S(2)}, u32[]{:S(2)}) collective-permute-start(f32[32,32,128]{2,1,0:T(8,128)S(1)} %pad_maximum_fusion.1), channel_id=1, source_target_pairs={{0,48},{16,0},{32,16},{48,32},{1,49},{17,1},{33,17},{49,33},{2,50}... | collective-permute-start | bytes 1572872 | tf_op jit(solution)/shard_map/ppermute | solution.py:343
  8.6 31.5 %collective-permute-start.7 = (f32[32,32,128]{2,1,0:T(8,128)S(1)}, f32[32,32,128]{2,1,0:T(8,128)S(1)}, u32[]{:S(2)}, u32[]{:S(2)}) collective-permute-start(f32[32,32,128]{2,1,0:T(8,128)S(1)} %get-tuple-element.88), channel_id=1, source_target_pairs={{0,48},{16,0},{32,16},{48,32},{1,49},{17,1},{33,17},{49,33},{2,50}... | collective-permute-start | bytes 1572872 | tf_op jit(solution)/shard_map/ppermute | solution.py:343
  10.1 42.3 %collective-permute-start.6 = (f32[32,32,128]{2,1,0:T(8,128)S(1)}, f32[32,32,128]{2,1,0:T(8,128)S(1)}, u32[]{:S(2)}, u32[]{:S(2)}) collective-permute-start(f32[32,32,128]{2,1,0:T(8,128)S(1)} %get-tuple-element.89), channel_id=1, source_target_pairs={{0,16},{16,32},{32,48},{48,0},{1,17},{17,33},{33,49},{49,1},{2,18}... | collective-permute-start | bytes 1572872 | tf_op jit(solution)/shard_map/ppermute | solution.py:343
  22.2 36.7 %collective-permute-start.5 = (f32[4,1,32,128]{3,2,1,0:T(8,128)}, f32[4,1,32,128]{3,2,1,0:T(8,128)S(1)}, u32[]{:S(2)}, u32[]{:S(2)}) collective-permute-start(f32[4,1,32,128]{3,2,1,0:T(8,128)} %get-tuple-element.90), channel_id=1, source_target_pairs={{0,12},{4,0},{8,4},{12,8},{1,13},{5,1},{9,5},{13,9},{2,14},{6,2},{... | collective-permute-start | bytes 196616 | tf_op jit(solution)/shard_map/ppermute | solution.py:349
  40.1 21.9 %collective-permute-start.4 = (f32[4,1,32,128]{3,2,1,0:T(8,128)}, f32[4,1,32,128]{3,2,1,0:T(8,128)S(1)}, u32[]{:S(2)}, u32[]{:S(2)}) collective-permute-start(f32[4,1,32,128]{3,2,1,0:T(8,128)} %get-tuple-element.91), channel_id=1, source_target_pairs={{0,4},{4,8},{8,12},{12,0},{1,5},{5,9},{9,13},{13,1},{2,6},{6,10},{... | collective-permute-start | bytes 196616 | tf_op jit(solution)/shard_map/ppermute | solution.py:348
  58.7 34.6 %collective-permute-start.14 = (f32[32,32,128]{2,1,0:T(8,128)}, f32[32,32,128]{2,1,0:T(8,128)S(1)}, u32[]{:S(2)}, u32[]{:S(2)}) collective-permute-start(f32[32,32,128]{2,1,0:T(8,128)} %get-tuple-element.55), channel_id=1, source_target_pairs={{0,16},{16,32},{32,48},{48,0},{1,17},{17,33},{33,49},{49,1},{2,18}... | collective-permute-start | bytes 1572872 | tf_op jit(solution)/shard_map/ppermute | solution.py:343
  58.8 34.5 %collective-permute-start.15 = (f32[32,32,128]{2,1,0:T(8,128)}, f32[32,32,128]{2,1,0:T(8,128)S(1)}, u32[]{:S(2)}, u32[]{:S(2)}) collective-permute-start(f32[32,32,128]{2,1,0:T(8,128)} %get-tuple-element.56), channel_id=1, source_target_pairs={{0,48},{16,0},{32,16},{48,32},{1,49},{17,1},{33,17},{49,33},{2,50}... | collective-permute-start | bytes 1572872 | tf_op jit(solution)/shard_map/ppermute | solution.py:343
  68.7 48.0 %collective-permute-start.8 = (f32[32,32,128]{2,1,0:T(8,128)}, f32[32,32,128]{2,1,0:T(8,128)S(1)}, u32[]{:S(2)}, u32[]{:S(2)}) collective-permute-start(f32[32,32,128]{2,1,0:T(8,128)} %get-tuple-element.49), channel_id=1, source_target_pairs={{0,16},{16,32},{32,48},{48,0},{1,17},{17,33},{33,49},{49,1},{2,18}... | collective-permute-start | bytes 1572872 | tf_op jit(solution)/shard_map/ppermute | solution.py:343
  68.8 47.9 %collective-permute-start.9 = (f32[32,32,128]{2,1,0:T(8,128)}, f32[32,32,128]{2,1,0:T(8,128)S(1)}, u32[]{:S(2)}, u32[]{:S(2)}) collective-permute-start(f32[32,32,128]{2,1,0:T(8,128)} %get-tuple-element.50), channel_id=1, source_target_pairs={{0,48},{16,0},{32,16},{48,32},{1,49},{17,1},{33,17},{49,33},{2,50}... | collective-permute-start | bytes 1572872 | tf_op jit(solution)/shard_map/ppermute | solution.py:343
  82.4 22.0 %collective-permute-start.12 = (f32[4,1,32,128]{3,2,1,0:T(8,128)}, f32[4,1,32,128]{3,2,1,0:T(8,128)S(1)}, u32[]{:S(2)}, u32[]{:S(2)}) collective-permute-start(f32[4,1,32,128]{3,2,1,0:T(8,128)} %get-tuple-element.53), channel_id=1, source_target_pairs={{0,4},{4,8},{8,12},{12,0},{1,5},{5,9},{9,13},{13,1},{2,6},{6,10},{... | collective-permute-start | bytes 196616 | tf_op jit(solution)/shard_map/ppermute | solution.py:348
  93.4 23.3 %collective-permute-start.13 = (f32[4,1,32,128]{3,2,1,0:T(8,128)}, f32[4,1,32,128]{3,2,1,0:T(8,128)S(1)}, u32[]{:S(2)}, u32[]{:S(2)}) collective-permute-start(f32[4,1,32,128]{3,2,1,0:T(8,128)} %get-tuple-element.54), channel_id=1, source_target_pairs={{0,12},{4,0},{8,4},{12,8},{1,13},{5,1},{9,5},{13,9},{2,14},{6,2},{... | collective-permute-start | bytes 196616 | tf_op jit(solution)/shard_map/ppermute | solution.py:349
  99.8 40.6 %collective-permute-start.16 = (f32[32,32,128]{2,1,0:T(8,128)}, f32[32,32,128]{2,1,0:T(8,128)S(1)}, u32[]{:S(2)}, u32[]{:S(2)}) collective-permute-start(f32[32,32,128]{2,1,0:T(8,128)} %get-tuple-element.61), channel_id=1, source_target_pairs={{0,16},{16,32},{32,48},{48,0},{1,17},{17,33},{33,49},{49,1},{2,18}... | collective-permute-start | bytes 1572872 | tf_op jit(solution)/shard_map/ppermute | solution.py:343
  104.4 36.0 %collective-permute-start.17 = (f32[32,32,128]{2,1,0:T(8,128)}, f32[32,32,128]{2,1,0:T(8,128)S(1)}, u32[]{:S(2)}, u32[]{:S(2)}) collective-permute-start(f32[32,32,128]{2,1,0:T(8,128)} %get-tuple-element.62), channel_id=1, source_target_pairs={{0,48},{16,0},{32,16},{48,32},{1,49},{17,1},{33,17},{49,33},{2,50}... | collective-permute-start | bytes 1572872 | tf_op jit(solution)/shard_map/ppermute | solution.py:343
  123.3 41.2 %collective-permute-start.20 = (f32[32,32,128]{2,1,0:T(8,128)}, f32[32,32,128]{2,1,0:T(8,128)S(1)}, u32[]{:S(2)}, u32[]{:S(2)}) collective-permute-start(f32[32,32,128]{2,1,0:T(8,128)} %get-tuple-element.66), channel_id=1, source_target_pairs={{0,16},{16,32},{32,48},{48,0},{1,17},{17,33},{33,49},{49,1},{2,18}... | collective-permute-start | bytes 1572872 | tf_op jit(solution)/shard_map/ppermute | solution.py:343
  124.1 40.4 %collective-permute-start.21 = (f32[32,32,128]{2,1,0:T(8,128)}, f32[32,32,128]{2,1,0:T(8,128)S(1)}, u32[]{:S(2)}, u32[]{:S(2)}) collective-permute-start(f32[32,32,128]{2,1,0:T(8,128)} %get-tuple-element.67), channel_id=1, source_target_pairs={{0,48},{16,0},{32,16},{48,32},{1,49},{17,1},{33,17},{49,33},{2,50}... | collective-permute-start | bytes 1572872 | tf_op jit(solution)/shard_map/ppermute | solution.py:343
  138.1 13.9 %collective-permute-start.22 = (f32[4,1,32,128]{3,2,1,0:T(8,128)}, f32[4,1,32,128]{3,2,1,0:T(8,128)S(1)}, u32[]{:S(2)}, u32[]{:S(2)}) collective-permute-start(f32[4,1,32,128]{3,2,1,0:T(8,128)} %get-tuple-element.68), channel_id=1, source_target_pairs={{0,4},{4,8},{8,12},{12,0},{1,5},{5,9},{9,13},{13,1},{2,6},{6,10},{... | collective-permute-start | bytes 196616 | tf_op jit(solution)/shard_map/ppermute | solution.py:348
  140.4 24.1 %collective-permute-start.23 = (f32[4,1,32,128]{3,2,1,0:T(8,128)}, f32[4,1,32,128]{3,2,1,0:T(8,128)S(1)}, u32[]{:S(2)}, u32[]{:S(2)}) collective-permute-start(f32[4,1,32,128]{3,2,1,0:T(8,128)} %get-tuple-element.69), channel_id=1, source_target_pairs={{0,12},{4,0},{8,4},{12,8},{1,13},{5,1},{9,5},{13,9},{2,14},{6,2},{... | collective-permute-start | bytes 196616 | tf_op jit(solution)/shard_map/ppermute | solution.py:349
  146.8 41.0 %collective-permute-start.24 = (f32[32,32,128]{2,1,0:T(8,128)}, f32[32,32,128]{2,1,0:T(8,128)S(1)}, u32[]{:S(2)}, u32[]{:S(2)}) collective-permute-start(f32[32,32,128]{2,1,0:T(8,128)} %get-tuple-element.73), channel_id=1, source_target_pairs={{0,16},{16,32},{32,48},{48,0},{1,17},{17,33},{33,49},{49,1},{2,18}... | collective-permute-start | bytes 1572872 | tf_op jit(solution)/shard_map/ppermute | solution.py:343
  152.0 35.8 %collective-permute-start.25 = (f32[32,32,128]{2,1,0:T(8,128)}, f32[32,32,128]{2,1,0:T(8,128)S(1)}, u32[]{:S(2)}, u32[]{:S(2)}) collective-permute-start(f32[32,32,128]{2,1,0:T(8,128)} %get-tuple-element.74), channel_id=1, source_target_pairs={{0,48},{16,0},{32,16},{48,32},{1,49},{17,1},{33,17},{49,33},{2,50}... | collective-permute-start | bytes 1572872 | tf_op jit(solution)/shard_map/ppermute | solution.py:343
  171.1 41.2 %collective-permute-start.28 = (f32[32,32,128]{2,1,0:T(8,128)}, f32[32,32,128]{2,1,0:T(8,128)S(1)}, u32[]{:S(2)}, u32[]{:S(2)}) collective-permute-start(f32[32,32,128]{2,1,0:T(8,128)} %get-tuple-element.78), channel_id=1, source_target_pairs={{0,16},{16,32},{32,48},{48,0},{1,17},{17,33},{33,49},{49,1},{2,18}... | collective-permute-start | bytes 1572872 | tf_op jit(solution)/shard_map/ppermute | solution.py:343
  171.7 40.6 %collective-permute-start.29 = (f32[32,32,128]{2,1,0:T(8,128)}, f32[32,32,128]{2,1,0:T(8,128)S(1)}, u32[]{:S(2)}, u32[]{:S(2)}) collective-permute-start(f32[32,32,128]{2,1,0:T(8,128)} %get-tuple-element.79), channel_id=1, source_target_pairs={{0,48},{16,0},{32,16},{48,32},{1,49},{17,1},{33,17},{49,33},{2,50}... | collective-permute-start | bytes 1572872 | tf_op jit(solution)/shard_map/ppermute | solution.py:343
  186.0 14.1 %collective-permute-start.30 = (f32[4,1,32,128]{3,2,1,0:T(8,128)}, f32[4,1,32,128]{3,2,1,0:T(8,128)S(1)}, u32[]{:S(2)}, u32[]{:S(2)}) collective-permute-start(f32[4,1,32,128]{3,2,1,0:T(8,128)} %get-tuple-element.80), channel_id=1, source_target_pairs={{0,4},{4,8},{8,12},{12,0},{1,5},{5,9},{9,13},{13,1},{2,6},{6,10},{... | collective-permute-start | bytes 196616 | tf_op jit(solution)/shard_map/ppermute | solution.py:348
  187.9 24.4 %collective-permute-start.31 = (f32[4,1,32,128]{3,2,1,0:T(8,128)}, f32[4,1,32,128]{3,2,1,0:T(8,128)S(1)}, u32[]{:S(2)}, u32[]{:S(2)}) collective-permute-start(f32[4,1,32,128]{3,2,1,0:T(8,128)} %get-tuple-element.81), channel_id=1, source_target_pairs={{0,12},{4,0},{8,4},{12,8},{1,13},{5,1},{9,5},{13,9},{2,14},{6,2},{... | collective-permute-start | bytes 196616 | tf_op jit(solution)/shard_map/ppermute | solution.py:349
  194.2 26.0 %collective-permute-start.41 = (f32[16,32,128]{2,1,0:T(8,128)}, f32[16,32,128]{2,1,0:T(8,128)S(1)}, u32[]{:S(2)}, u32[]{:S(2)}) collective-permute-start(f32[16,32,128]{2,1,0:T(8,128)} %get-tuple-element.86), channel_id=1, source_target_pairs={{0,16},{1,17},{2,18},{3,19},{4,20},{5,21},{6,22},{7,23},{8,24},{9,... | collective-permute-start | bytes 786440 | tf_op jit(solution)/shard_map/ppermute | solution.py:409
  200.1 20.8 %collective-permute-start.44 = (f32[16,32,128]{2,1,0:T(8,128)}, f32[16,32,128]{2,1,0:T(8,128)S(1)}, u32[]{:S(2)}, u32[]{:S(2)}) collective-permute-start(f32[16,32,128]{2,1,0:T(8,128)} %get-tuple-element.87), channel_id=1, source_target_pairs={{0,16},{1,17},{2,18},{3,19},{4,20},{5,21},{6,22},{7,23},{8,24},{9,... | collective-permute-start | bytes 786440 | tf_op jit(solution)/shard_map/ppermute | solution.py:409
  218.7 7.8 %collective-permute-start.32 = (f32[16,32,128]{2,1,0:T(8,128)}, f32[16,32,128]{2,1,0:T(8,128)S(1)}, u32[]{:S(2)}, u32[]{:S(2)}) collective-permute-start(f32[16,32,128]{2,1,0:T(8,128)} %get-tuple-element.83), channel_id=1, source_target_pairs={{0,16},{1,17},{2,18},{3,19},{4,20},{5,21},{6,22},{7,23},{8,24},{9,... | collective-permute-start | bytes 786440 | tf_op jit(solution)/shard_map/ppermute | solution.py:409
  220.3 14.0 %collective-permute-start.42 = (f32[16,32,128]{2,1,0:T(8,128)S(1)}, f32[16,32,128]{2,1,0:T(8,128)S(1)}, u32[]{:S(2)}, u32[]{:S(2)}) collective-permute-start(f32[16,32,128]{2,1,0:T(8,128)S(1)} %add.36), channel_id=1, source_target_pairs={{16,32},{17,33},{18,34},{19,35},{20,36},{21,37},{22,38},{23,39},{2... | collective-permute-start | bytes 786440 | tf_op jit(solution)/shard_map/ppermute | solution.py:409
  221.0 14.0 %collective-permute-start.45 = (f32[16,32,128]{2,1,0:T(8,128)S(1)}, f32[16,32,128]{2,1,0:T(8,128)S(1)}, u32[]{:S(2)}, u32[]{:S(2)}) collective-permute-start(f32[16,32,128]{2,1,0:T(8,128)S(1)} %add.38), channel_id=1, source_target_pairs={{16,32},{17,33},{18,34},{19,35},{20,36},{21,37},{22,38},{23,39},{2... | collective-permute-start | bytes 786440 | tf_op jit(solution)/shard_map/ppermute | solution.py:409
  227.6 11.6 %collective-permute-start.33 = (f32[16,32,128]{2,1,0:T(8,128)S(1)}, f32[16,32,128]{2,1,0:T(8,128)S(1)}, u32[]{:S(2)}, u32[]{:S(2)}) collective-permute-start(f32[16,32,128]{2,1,0:T(8,128)S(1)} %add.30), channel_id=1, source_target_pairs={{16,32},{17,33},{18,34},{19,35},{20,36},{21,37},{22,38},{23,39},{2... | collective-permute-start | bytes 786440 | tf_op jit(solution)/shard_map/ppermute | solution.py:409
  228.3 7.5 %collective-permute-start.35 = (f32[8,32,128]{2,1,0:T(8,128)}, f32[8,32,128]{2,1,0:T(8,128)S(1)}, u32[]{:S(2)}, u32[]{:S(2)}) collective-permute-start(f32[8,32,128]{2,1,0:T(8,128)} %get-tuple-element.84), channel_id=1, source_target_pairs={{0,16},{1,17},{2,18},{3,19},{4,20},{5,21},{6,22},{7,23},{8,24},{9,... | collective-permute-start | bytes 393224 | tf_op jit(solution)/shard_map/ppermute | solution.py:409
  234.3 7.7 %collective-permute-start.43 = (f32[16,32,128]{2,1,0:T(8,128)S(1)}, f32[16,32,128]{2,1,0:T(8,128)S(1)}, u32[]{:S(2)}, u32[]{:S(2)}) collective-permute-start(f32[16,32,128]{2,1,0:T(8,128)S(1)} %add.37), channel_id=1, source_target_pairs={{32,48},{33,49},{34,50},{35,51},{36,52},{37,53},{38,54},{39,55},{4... | collective-permute-start | bytes 786440 | tf_op jit(solution)/shard_map/ppermute | solution.py:409
  (67 other events, 453.9 us)
